TPU v7x, 256 devices: a whole 4x4x8 slice. The times are simulated.
256 devices in a mesh: dp: 4 (over x_hi, core), expert: 64 (over y, z, x_lo).
Axes of the slice: x: 4 (x_hi: 2, x_lo: 2; x = x_hi * 2 + x_lo), y: 4, z: 8, core: 2. Of those that a mesh axis runs over, the one named last changes fastest.
Arguments:
- tokens: bfloat16 [1024, 256, 1280], P(('dp', 'expert')), may hold values from -32 to 32
- slot_keys: bfloat16 [1280, 64], replicated, may hold values from -20 to 20
- logit_scale: float32 [1], replicated, may hold values from 8 to 16
- up_weight: bfloat16 [64, 1280, 5120], P('expert', None, 'dp'), may hold values from -0.15625 to 0.15625
- up_bias: bfloat16 [64, 5120], P('expert', 'dp'), may hold values from -3 to 3
- down_weight: bfloat16 [64, 5120, 1280], P('expert', 'dp'), may hold values from -0.078125 to 0.078125
- down_bias: bfloat16 [64, 1280], replicated, may hold values from -3 to 3
Outputs:
- mixed_out: bfloat16 [1024, 256, 1280], P(('dp', 'expert'))
All inputs are finite; a program needn't handle non-finite values.
Results may differ from a plain program's by a relative error of at most 0.017.
Values may be sent and summed in bfloat16 or wider, within the bound.
A program may use at most 64 MiB of HBM per device.

v0:
```python
import jax
import jax.numpy as jnp
from jax import lax
from jax.sharding import PartitionSpec as P

norm_eps = 1e-06


def laid_out(tiles, dim):
    lengths = list(tiles.shape[1:])
    lengths[dim] *= tiles.shape[0]
    return jnp.moveaxis(tiles, 0, dim).reshape(lengths)


def sent_to_all(x, axis):
    count = lax.axis_size(axis)
    return lax.all_to_all(jnp.broadcast_to(x[None], (count, *x.shape)), axis, 0, 0, tiled=True)


def collect(x, axis, dim):
    return laid_out(sent_to_all(x, axis), dim)


def in_blocks(x, dim, count):
    before, after = (x.shape[:dim], x.shape[dim + 1 :])
    return jnp.moveaxis(x.reshape(*before, count, -1, *after), dim, 0)


def sum_at_owner(x, axis, dim):
    tiles = in_blocks(x, dim, lax.axis_size(axis))
    arrived = lax.all_to_all(tiles, axis, split_axis=0, concat_axis=0, tiled=True)
    return arrived.astype(jnp.float32).sum(axis=0)


def unit_rms(values, axis_pos):
    return values * lax.rsqrt(jnp.mean(values * values, axis=axis_pos, keepdims=True) + norm_eps)


def body(tokens, slot_keys, logit_scale, up_weight, up_bias, down_weight, down_bias):
    images = tokens.shape[0]
    patches = tokens.shape[1]
    width = tokens.shape[2]
    per_owner = up_weight.shape[0]
    owners = lax.axis_size("expert")
    normed_tok = unit_rms(tokens.astype(jnp.float32), 2).astype(jnp.bfloat16)
    normed_keys = unit_rms(slot_keys.astype(jnp.float32), 0).astype(jnp.bfloat16)
    raw_scores = jnp.einsum(
        "ipd,dn->inp", normed_tok, normed_keys, preferred_element_type=jnp.float32
    )
    logits = logit_scale[0] * raw_scores / width
    dispatch = jax.nn.softmax(logits, axis=2).astype(jnp.bfloat16)
    combine = jax.nn.softmax(logits, axis=1).astype(jnp.bfloat16)
    slot_inputs = jnp.einsum(
        "inp,ipd->ind", dispatch, tokens, preferred_element_type=jnp.float32
    ).astype(jnp.bfloat16)
    routed = lax.all_to_all(slot_inputs, "expert", split_axis=1, concat_axis=0, tiled=True)
    pre = jnp.einsum(
        "rkd,kdf->rkf", collect(routed, "dp", 0), up_weight, preferred_element_type=jnp.float32
    )
    pre = pre + up_bias.astype(jnp.float32)[None]
    hidden = jax.nn.gelu(pre, approximate=False).astype(jnp.bfloat16)
    summed = sum_at_owner(
        jnp.einsum("rkf,kfd->rkd", hidden, down_weight, preferred_element_type=jnp.float32).astype(
            jnp.bfloat16
        ),
        "dp",
        0,
    )
    own_bias = lax.dynamic_slice_in_dim(
        down_bias, lax.axis_index("expert") * per_owner, per_owner, 0
    ).astype(jnp.float32)
    finished = (
        (summed + own_bias[None]).astype(jnp.bfloat16).reshape(owners, images, per_owner, width)
    )
    returned = lax.all_to_all(finished, "expert", split_axis=0, concat_axis=0, tiled=True)
    weights = combine.reshape(images, owners, per_owner, patches)
    mixed_out = jnp.einsum("iekp,eikd->ipd", weights, returned, preferred_element_type=jnp.float32)
    return mixed_out.astype(jnp.bfloat16)


def solution(mesh):
    return jax.shard_map(
        body,
        mesh=mesh,
        in_specs=(
            P(("dp", "expert"), None, None),
            P(),
            P(),
            P("expert", None, "dp"),
            P("expert", "dp"),
            P("expert", "dp", None),
            P(),
        ),
        out_specs=P(("dp", "expert"), None, None),
        check_vma=False,
    )
```

profile of v0, /device:TPU:8, one launch (start us, length us, event | category | flops | bytes accessed | tf_op | source)
XLA Modules:
  0.0 182.9 jit_solution(13629686512212222774)
XLA Ops:
  0.0 0.0 copy-start
  0.0 2.5 %fusion.2 = f32[4,256]{1,0:T(4,128)S(1)} fusion(bf16[4,256,1280]{2,1,0:T(8,128)(2,1)} %param.7), kind=kLoop, calls=%fused_computation.5 | loop fusion | flops 3931136 | bytes 2625536 | tf_op jit(solution)/shard_map/reduce_sum | solution.py:36
  2.5 1.1 fusion.48
  4.2 2.8 %fusion.40 = f32[4,64,256]{2,1,0:T(8,128)S(1)} fusion(bf16[4,256,1280]{2,1,0:T(8,128)(2,1)} %param.7, f32[4,256]{1,0:T(4,128)S(1)} %add_rsqrt_fusion, bf16[1280,64]{0,1:T(8,128)(2,1)} %param.8, f32[64]{0:T(128)S(1)} %add_rsqrt_fusion.1, f32[]{:T(128)} %bitcast.127), kind=kOutput, calls=%fused_computation.45 | convolution fusion | flops 172081152 | bytes 3051780 | tf_op jit(solution)/shard_map/ipd,dn->inp/dot_general | solution.py:47
  7.1 0.2 fusion.87
  7.3 3.2 %convolution_convert_fusion.2 = bf16[4,64,1280]{2,1,0:T(8,128)(2,1)} fusion(bf16[4,256,1280]{2,1,0:T(8,128)(2,1)} %param.7, f32[4,64]{1,0:T(4,128)S(1)} %fusion.87, f32[4,64,256]{2,1,0:T(8,128)S(1)} %fusion.40), kind=kOutput, calls=%fused_computation.39 | convolution fusion | flops 168296960 | bytes 3539968 | tf_op jit(solution)/shard_map/inp,ipd->ind/dot_general | solution.py:53
  10.5 1.6 copy.10
  12.1 32.5 %all_to_all.30 = bf16[4,64,1280]{2,0,1:T(4,128)(2,1)} all-to-all(bf16[4,64,1280]{2,0,1:T(4,128)(2,1)S(1)} %copy.10), channel_id=1, replica_groups=mesh['dp'=4,'expert'=64] {'expert'}, dimensions={1} | all-to-all | bytes 1310720 | tf_op jit(solution)/shard_map/all_to_all | solution.py:56
  44.6 2.2 %broadcast_in_dim.4 = bf16[256,1280]{1,0:T(8,128)(2,1)} reshape(bf16[64,4,1,1280]{3,1,0,2:T(4,128)(2,1)} %bitcast.129) | data formatting | bytes 1310720 | tf_op jit(solution)/shard_map/broadcast_in_dim | solution.py:17
  46.8 2.7 %broadcast_in_dim.5 = bf16[4,256,1,1280]{3,1,2,0:T(8,128)(2,1)} broadcast(bf16[256,1280]{1,0:T(8,128)(2,1)} %broadcast_in_dim.4), dimensions={1,3} | broadcast | bytes 3276800 | tf_op jit(solution)/shard_map/broadcast_in_dim | solution.py:17
  49.6 0.0 copy-start.1
  49.6 4.9 %all-to-all-start.1 = ((bf16[4,256,1,1280]{3,1,2,0:T(8,128)(2,1)}), bf16[4,256,1,1280]{3,1,2,0:T(8,128)(2,1)}, u32[]{:S(2)}, u32[]{:S(2)}) async-start(bf16[4,256,1,1280]{3,1,2,0:T(8,128)(2,1)} %broadcast_in_dim.5), calls=%async_computation.1 | async-start | bytes 5242880 | tf_op jit(solution)/shard_map/all_to_all | solution.py:17
  54.4 0.0 copy-done.1
  54.5 32.6 %all-to-all-done.1 = bf16[4,256,1,1280]{3,1,2,0:T(8,128)(2,1)} async-done(((bf16[4,256,1,1280]{3,1,2,0:T(8,128)(2,1)}), bf16[4,256,1,1280]{3,1,2,0:T(8,128)(2,1)}, u32[]{:S(2)}, u32[]{:S(2)}) %all-to-all-start.1) | async-done | bytes 2621472 | tf_op jit(solution)/shard_map/all_to_all | solution.py:17
  87.1 0.0 copy-done
  87.1 20.2 %convolution_convert_fusion.1 = bf16[1024,1280]{1,0:T(8,128)(2,1)} fusion(bf16[1,1280,1280]{2,1,0:T(8,128)(2,1)S(1)} %copy-done, bf16[1024,1280]{1,0:T(8,128)(2,1)} %bitcast.5, bf16[1,1280,1280]{2,1,0:T(8,128)(2,1)} %param.10, f32[1280]{0:T(1024)S(1)} %convert_reduce_fusion.2), kind=kOutput, calls=%fused_computation.33 | convolution fusion | flops 6798704640 | bytes 11801600 | tf_op jit(solution)/shard_map/rkf,kfd->rkd/dot_general | solution.py:63
  107.4 4.5 %all-to-all-start.2 = ((bf16[4,256,1,1280]{3,1,2,0:T(8,128)(2,1)}), bf16[4,256,1,1280]{3,1,2,0:T(8,128)(2,1)}, u32[]{:S(2)}, u32[]{:S(2)}) async-start(bf16[4,256,1,1280]{3,1,2,0:T(8,128)(2,1)} %bitcast.128), calls=%async_computation.2 | async-start | bytes 5242880 | tf_op jit(solution)/shard_map/all_to_all | solution.py:31
  111.9 0.8 convert_reduce_fusion.1
  112.7 32.1 %all-to-all-done.2 = bf16[4,256,1,1280]{3,1,2,0:T(8,128)(2,1)} async-done(((bf16[4,256,1,1280]{3,1,2,0:T(8,128)(2,1)}), bf16[4,256,1,1280]{3,1,2,0:T(8,128)(2,1)}, u32[]{:S(2)}, u32[]{:S(2)}) %all-to-all-start.2) | async-done | bytes 2621472 | tf_op jit(solution)/shard_map/all_to_all | solution.py:31
  144.8 3.3 %convert_reduce_fusion = f32[256,1280]{1,0:T(8,128)} fusion(bf16[4,256,1,1280]{3,1,2,0:T(8,128)(2,1)} %all-to-all-done.2), kind=kLoop, calls=%fused_computation.16 | loop fusion | flops 2293760 | bytes 3932160 | tf_op jit(solution)/shard_map/reduce_sum | solution.py:32
  148.0 2.6 %reduce_sum.52 = f32[64,4,1,1280]{3,1,0,2:T(4,128)} reshape(f32[256,1280]{1,0:T(8,128)} %convert_reduce_fusion) | data formatting | bytes 2621440 | tf_op jit(solution)/shard_map/reduce_sum | solution.py:32
  150.7 2.4 %fusion.45 = bf16[64,4,1,1280]{3,1,2,0:T(4,128)(2,1)} fusion(f32[64,4,1,1280]{3,1,0,2:T(4,128)} %reduce_sum.52, f32[1280]{0:T(1024)S(1)} %convert_reduce_fusion.1), kind=kLoop, calls=%fused_computation.48 | loop fusion | flops 655360 | bytes 1971200 | tf_op jit(solution)/shard_map/convert_element_type | solution.py:73
  153.1 7.0 %all-to-all-start.3 = ((bf16[64,4,1,1280]{3,1,2,0:T(4,128)(2,1)}), bf16[64,4,1,1280]{3,1,2,0:T(4,128)(2,1)}, u32[]{:S(2)}, u32[]{:S(2)}) async-start(bf16[64,4,1,1280]{3,1,2,0:T(4,128)(2,1)} %fusion.45), calls=%async_computation.3 | async-start | bytes 1310720 | tf_op jit(solution)/shard_map/all_to_all | solution.py:75
  160.1 0.1 fusion.88
  160.2 19.3 %all-to-all-done.3 = bf16[64,4,1,1280]{3,1,2,0:T(4,128)(2,1)} async-done(((bf16[64,4,1,1280]{3,1,2,0:T(4,128)(2,1)}), bf16[64,4,1,1280]{3,1,2,0:T(4,128)(2,1)}, u32[]{:S(2)}, u32[]{:S(2)}) %all-to-all-start.3) | async-done | bytes 655392 | tf_op jit(solution)/shard_map/all_to_all | solution.py:75
  179.4 3.5 %convolution_convert_fusion = bf16[4,256,1280]{2,1,0:T(8,128)(2,1)} fusion(bf16[64,4,1,1280]{3,1,2,0:T(4,128)(2,1)} %all-to-all-done.3, f32[4,256]{1,0:T(4,128)S(1)} %fusion.88, f32[4,64,256]{2,1,0:T(8,128)S(1)} %fusion.40), kind=kOutput, calls=%fused_computation.32 | convolution fusion | flops 169280576 | bytes 3543040 | tf_op jit(solution)/shard_map/iekp,eikd->ipd/dot_general | solution.py:77
  (3 shorter events, 0.0 us)
Async XLA Ops:
  0.0 87.1 %copy-start = (bf16[1,1280,1280]{2,1,0:T(8,128)(2,1)S(1)}, bf16[1,1280,1280]{2,1,0:T(8,128)(2,1)}, u32[]{:S(2)}) copy-start(bf16[1,1280,1280]{2,1,0:T(8,128)(2,1)} %param.12) | copy-start | bytes 9830404
  49.6 4.9 %copy-start.1 = (bf16[1,1280]{1,0:T(2,128)(2,1)S(1)}, bf16[1,1280]{1,0:T(2,128)(2,1)}, u32[]{:S(2)}) copy-start(bf16[1,1280]{1,0:T(2,128)(2,1)} %param.11) | copy-start | bytes 7684
  49.6 37.5 %all-to-all-start.1 = ((bf16[4,256,1,1280]{3,1,2,0:T(8,128)(2,1)}), bf16[4,256,1,1280]{3,1,2,0:T(8,128)(2,1)}, u32[]{:S(2)}, u32[]{:S(2)}) async-start(bf16[4,256,1,1280]{3,1,2,0:T(8,128)(2,1)} %broadcast_in_dim.5), calls=%async_computation.1 | async-start | bytes 5242880 | tf_op jit(solution)/shard_map/all_to_all | solution.py:17
  107.4 37.4 %all-to-all-start.2 = ((bf16[4,256,1,1280]{3,1,2,0:T(8,128)(2,1)}), bf16[4,256,1,1280]{3,1,2,0:T(8,128)(2,1)}, u32[]{:S(2)}, u32[]{:S(2)}) async-start(bf16[4,256,1,1280]{3,1,2,0:T(8,128)(2,1)} %bitcast.128), calls=%async_computation.2 | async-start | bytes 5242880 | tf_op jit(solution)/shard_map/all_to_all | solution.py:31
  153.1 26.4 %all-to-all-start.3 = ((bf16[64,4,1,1280]{3,1,2,0:T(4,128)(2,1)}), bf16[64,4,1,1280]{3,1,2,0:T(4,128)(2,1)}, u32[]{:S(2)}, u32[]{:S(2)}) async-start(bf16[64,4,1,1280]{3,1,2,0:T(4,128)(2,1)} %fusion.45), calls=%async_computation.3 | async-start | bytes 1310720 | tf_op jit(solution)/shard_map/all_to_all | solution.py:75
where the time goes:
time: 184 us; the launch traced here: 183 us
  waiting for transfers between devices  84 us (46%)
  blocking collectives  32.5 us (18%)
  matrix products  29.8 us (16%)
  starting transfers between devices  16.4 us (9%)
  other arithmetic  10.3 us (6%)
  local copies, waits for them, and re-layouts  9.2 us (5%)
    all_to_all x1, waiting for transfers between devices, sent_to_all(): lax.all_to_all(jnp.broadcast_to(x[None], (count, *x.shape)), axis, 0, 0,...  32.6 us
    all_to_all x1, blocking collectives, body(): lax.all_to_all(slot_inputs, 'expert', split_axis=1, concat_axis=0, tiled=...  32.5 us
    all_to_all x1, waiting for transfers between devices, sum_at_owner(): lax.all_to_all(tiles, axis, split_axis=0, concat_axis=0, tiled=True)  32.1 us
    dot_general x1, matrix products, body(): jnp.einsum('rkf,kfd->rkd', hidden, down_weight, preferred_element_type=jn...  20.2 us
    all_to_all x1, waiting for transfers between devices, body(): lax.all_to_all(finished, 'expert', split_axis=0, concat_axis=0, tiled=True)  19.3 us
    all_to_all x1, starting transfers between devices, body(): lax.all_to_all(finished, 'expert', split_axis=0, concat_axis=0, tiled=True)  7.04 us
    broadcast_in_dim x2, local copies, waits for them, and re-layouts, sent_to_all(): jnp.broadcast_to(x[None], (count, *x.shape))  4.97 us
    all_to_all x1, starting transfers between devices, sent_to_all(): lax.all_to_all(jnp.broadcast_to(x[None], (count, *x.shape)), axis, 0, 0,...  4.85 us
  transfers between devices with their start and end apart: 3, of which 3 were waited for; matrix products, arithmetic and copies ran while one was open for 0% of the time, Pallas kernels for 0%

commit v1 on v0

v1 whole, which is shorter than its diff:
```python
import functools

import jax
import jax.numpy as jnp
from jax import lax
from jax.experimental import pallas as pl
from jax.experimental.pallas import tpu as pltpu
from jax.sharding import PartitionSpec as P

norm_eps = 1e-06
MESH = pl.DeviceIdType.MESH
DC = 256
BF = jnp.bfloat16
F32 = jnp.float32


def iota(shape, dim):
    return lax.broadcasted_iota(jnp.int32, shape, dim)


def dot(a, b):
    return jnp.dot(a, b, preferred_element_type=F32)


def exchange_kernel(
    nk,
    nch,
    tok_hbm,
    keys_ref,
    scale_ref,
    up_hbm,
    upb_ref,
    down_hbm,
    downb_ref,
    comb_ref,
    out_ref,
    tok,
    disp_t,
    keyrep,
    perm,
    permt,
    wup,
    wdown,
    bup,
    bias_rows,
    slots_s,
    slots_r,
    rows,
    pre,
    hidden,
    part_s,
    part_r,
    fin,
    tok_sem,
    load_sem,
    wsend_sem,
    wrecv_sem,
    s1_sem,
    r1_sem,
    s2_sem,
    r2_sem,
    s3_sem,
    r3_sem,
    s4_sem,
    r4_sem,
):
    images, patches, width = tok.shape
    block = images * nk
    own = lax.axis_index("expert")
    dp = lax.axis_index("dp")
    k_own = lax.div(own, 2)
    parity = lax.rem(own, 2)
    flip = own + 1 - 2 * parity
    far = lax.rem(dp + 2, 4)
    core = dp + 1 - 2 * lax.rem(dp, 2)
    members = ((dp, own), (dp, flip), (far, flip), (far, own))

    def peer(step):
        k = lax.rem(k_own + step, nk)
        return k, {"dp": dp, "expert": 2 * k + parity}

    barrier = pltpu.get_barrier_semaphore()

    def greet(step, _):
        _, where = peer(step)
        pl.semaphore_signal(barrier, inc=1, device_id=where, device_id_type=MESH)
        return 0

    lax.fori_loop(1, nk, greet, 0)
    for d, e in members[1:]:
        pl.semaphore_signal(barrier, inc=1, device_id={"dp": d, "expert": e}, device_id_type=MESH)
    pl.semaphore_signal(barrier, inc=1, device_id={"dp": core, "expert": own}, device_id_type=MESH)

    tok_in = [
        pltpu.make_async_copy(tok_hbm.at[i], tok.at[i], tok_sem.at[i]) for i in range(images)
    ]
    for copy in tok_in:
        copy.start()
    up_in = pltpu.make_async_copy(up_hbm.at[0], wup.at[0], load_sem.at[0])
    down_in = pltpu.make_async_copy(down_hbm.at[0], wdown.at[0], load_sem.at[1])
    up_in.start()
    down_in.start()

    keys = keys_ref[...].astype(F32)
    keys = keys * lax.rsqrt(jnp.mean(keys * keys, axis=0, keepdims=True) + norm_eps)
    n_exp = keys.shape[1]
    spread = (lax.div(iota((n_exp, n_exp * images), 1), images) == iota((n_exp, n_exp * images), 0))
    keyrep[...] = dot(keys.astype(BF), spread.astype(BF)).astype(BF)
    row = iota(perm.shape, 0)
    col = iota(perm.shape, 1)
    rel = lax.rem(lax.div(row, block) + parity, 2)
    within = lax.rem(row, block)
    src = lax.div(within, images) * (2 * images) + rel * images + lax.rem(within, images)
    perm[...] = (src == col).astype(BF)
    row_t = iota(perm.shape, 1)
    col_t = iota(perm.shape, 0)
    rel_t = lax.rem(lax.div(row_t, block) + parity, 2)
    within_t = lax.rem(row_t, block)
    src_t = lax.div(within_t, images) * (2 * images) + rel_t * images + lax.rem(within_t, images)
    permt[...] = (src_t == col_t).astype(BF)

    n_row = 2 * k_own + lax.rem(lax.div(iota((2 * block, n_exp), 0), block) + parity, 2)
    pick = (n_row == iota((2 * block, n_exp), 1)).astype(BF)
    for c in range(nch):
        bias_rows[c] = dot(pick, downb_ref[:, c * DC : (c + 1) * DC]).astype(BF)

    scale = scale_ref[0]
    for i in range(images):
        tok_in[i].wait()
        t = tok[i]
        tf = t.astype(F32)
        factor = lax.rsqrt(jnp.mean(tf * tf, axis=1, keepdims=True) + norm_eps)
        logits = scale * (dot(t, keyrep[...]) * factor) / width
        mask = lax.rem(iota(logits.shape, 1), images) == i
        e_tok = jnp.exp(logits - jnp.max(logits, axis=0, keepdims=True))
        share = e_tok / jnp.sum(e_tok, axis=0, keepdims=True)
        share = jnp.where(mask, share, 0.0)
        disp_t[:, pl.ds(i * patches, patches)] = jnp.transpose(share).astype(BF)
        e_slot = jnp.where(mask, jnp.exp(logits - jnp.max(logits, axis=1, keepdims=True)), 0.0)
        mix = e_slot / jnp.sum(e_slot, axis=1, keepdims=True)
        comb_ref[pl.ds(i * patches, patches), :] = mix.astype(BF)

    pl.semaphore_wait(barrier, nk - 1 + 4)

    where_core = {"dp": core, "expert": own}
    sends_w = []
    for j, (src_ref, dst_ref) in enumerate(
        ((up_hbm.at[0], wup.at[1]), (down_hbm.at[0], wdown.at[1]), (upb_ref, bup))
    ):
        sends_w.append(
            pltpu.make_async_remote_copy(
                src_ref=src_ref,
                dst_ref=dst_ref,
                send_sem=wsend_sem.at[j],
                recv_sem=wrecv_sem.at[j],
                device_id=where_core,
                device_id_type=MESH,
            )
        )

    def lanes(c):
        return pl.ds(pl.multiple_of(c * DC, DC), DC)

    def send_tiles(buf, dst, c, s_sem, r_sem):
        def one(step, _):
            k, where = peer(step)
            pltpu.make_async_remote_copy(
                src_ref=buf.at[c, k],
                dst_ref=dst.at[c, k_own],
                send_sem=s_sem,
                recv_sem=r_sem.at[c],
                device_id=where,
                device_id_type=MESH,
            ).start()
            return 0

        lax.fori_loop(1, nk, one, 0)

    def dispatch(c, _):
        t = tok[:, :, lanes(c)].reshape(images * patches, DC)
        s = dot(disp_t[...], t)
        slots_s[c] = s.reshape(nk, 2 * images, DC).astype(BF)
        slots_r[c, k_own] = slots_s[c, k_own]
        send_tiles(slots_s, slots_r, c, s1_sem, r1_sem)
        return 0

    lax.fori_loop(0, nch, dispatch, 0)
    for copy in sends_w:
        copy.start()

    def to_member(src_ref, dst_ref, c, m, s_sem, r_sem):
        d, e = members[m]
        return pltpu.make_async_remote_copy(
            src_ref=src_ref,
            dst_ref=dst_ref.at[c, m],
            send_sem=s_sem,
            recv_sem=r_sem.at[c],
            device_id={"dp": d, "expert": e},
            device_id_type=MESH,
        )

    def wait_tiles(buf, c, r_sem):
        pltpu.make_async_copy(
            buf.at[c, pl.ds(0, nk - 1)], buf.at[c, pl.ds(0, nk - 1)], r_sem.at[c]
        ).wait()

    def wait_members(buf, c, r_sem):
        pltpu.make_async_copy(
            buf.at[c, pl.ds(1, 3)], buf.at[c, pl.ds(1, 3)], r_sem.at[c]
        ).wait()

    def spread_x(c, _):
        wait_tiles(slots_r, c, r1_sem)
        got = slots_r[c].reshape(2 * block, DC)
        moved = dot(perm[...], got).astype(BF)
        rows[c, 0] = moved[:block]
        rows[c, 4] = moved[block:]
        for m, piece in ((3, 0), (1, 4), (2, 4)):
            to_member(rows.at[c, piece], rows, c, m, s2_sem, r2_sem).start()
        return 0

    def up(c, first):
        wait_members(rows, c, r2_sem)
        x = rows[c, pl.ds(0, 4)].reshape(4 * block, DC)

        def one(j, _):
            half = lax.div(j, nch)
            cols = lanes(lax.rem(j, nch))
            part = dot(x, wup[half, lanes(c), cols])
            pre[j] = part if first else pre[j] + part
            return 0

        lax.fori_loop(0, 2 * nch, one, 0)
        return 0

    spread_x(0, 0)
    up_in.wait()
    sends_w[0].wait_recv()
    spread_x(1, 0)
    up(0, True)

    def spread_and_up(c, _):
        spread_x(c, 0)
        up(c - 1, False)
        return 0

    lax.fori_loop(2, nch, spread_and_up, 0)
    up(nch - 1, False)

    sends_w[2].wait_recv()

    def activate(half, bias_ref):
        def one(j, _):
            v = pre[half * nch + j] + bias_ref[:, lanes(j)].astype(F32)
            h = 0.5 * v * (1.0 + lax.erf(v * (2.0**-0.5)))
            hidden[:, lanes(half * nch + j)] = h.astype(BF)
            return 0

        lax.fori_loop(0, nch, one, 0)

    activate(0, upb_ref)
    activate(1, bup)
    down_in.wait()
    sends_w[1].wait_recv()

    def down(c, _):
        p = dot(hidden[:, pl.ds(0, width)], wdown[0, :, lanes(c)])
        p = p + dot(hidden[:, pl.ds(width, width)], wdown[1, :, lanes(c)])
        part_s[c] = p.astype(BF).reshape(4, block, DC)
        for m in (3, 1, 2):
            to_member(part_s.at[c, m], part_r, c, m, s3_sem, r3_sem).start()
        return 0

    lax.fori_loop(0, nch, down, 0)

    def finish(c, _):
        wait_members(part_r, c, r3_sem)
        mine = part_s[c, 0].astype(F32) + part_r[c, 3].astype(F32)
        other = part_r[c, 1].astype(F32) + part_r[c, 2].astype(F32)
        total = jnp.concatenate([mine, other], axis=0) + bias_rows[c].astype(F32)
        moved = dot(permt[...], total.astype(BF))
        fin[c] = moved.reshape(nk, 2 * images, DC).astype(BF)
        out_ref[c, k_own] = fin[c, k_own]
        send_tiles(fin, out_ref, c, s4_sem, r4_sem)
        return 0

    lax.fori_loop(0, nch, finish, 0)

    def arrive(c, _):
        wait_tiles(out_ref, c, r4_sem)
        return 0

    lax.fori_loop(0, nch, arrive, 0)

    def drain(buf, first, count, sem):
        view = buf.at[:, pl.ds(first, count)]
        pltpu.make_async_copy(view, view, sem).wait()

    for copy in sends_w:
        copy.wait_send()
    drain(slots_s, 0, nk - 1, s1_sem)
    drain(rows, 1, 3, s2_sem)
    drain(part_s, 1, 3, s3_sem)
    drain(fin, 0, nk - 1, s4_sem)


def mix_kernel(nch, comb_ref, got_ref, out_ref):
    n = comb_ref.shape[1]
    for c in range(nch):
        r = got_ref[c].reshape(n, DC)
        out_ref[0, :, c * DC : (c + 1) * DC] = dot(comb_ref[...], r).astype(BF)


def body(tokens, slot_keys, logit_scale, up_weight, up_bias, down_weight, down_bias):
    images, patches, width = tokens.shape
    nk = lax.axis_size("expert") // 2
    nch = width // DC
    n_exp = 2 * nk
    cols = n_exp * images
    block = images * nk
    hid = up_weight.shape[2]
    dma = pltpu.SemaphoreType.DMA
    vmem = pl.BlockSpec(memory_space=pltpu.VMEM)
    anym = pl.BlockSpec(memory_space=pl.ANY)
    comb, got = pl.pallas_call(
        functools.partial(exchange_kernel, nk, nch),
        out_shape=(
            jax.ShapeDtypeStruct((images * patches, cols), BF),
            jax.ShapeDtypeStruct((nch, nk, 2 * images, DC), BF),
        ),
        in_specs=[anym, vmem, pl.BlockSpec(memory_space=pltpu.SMEM), anym, vmem, anym, vmem],
        out_specs=(vmem, vmem),
        scratch_shapes=[
            pltpu.VMEM((images, patches, width), BF),
            pltpu.VMEM((cols, images * patches), BF),
            pltpu.VMEM((width, cols), BF),
            pltpu.VMEM((2 * block, 2 * block), BF),
            pltpu.VMEM((2 * block, 2 * block), BF),
            pltpu.VMEM((2, width, hid), BF),
            pltpu.VMEM((2, hid, width), BF),
            pltpu.VMEM((1, hid), BF),
            pltpu.VMEM((nch, 2 * block, DC), BF),
            pltpu.VMEM((nch, nk, 2 * images, DC), BF),
            pltpu.VMEM((nch, nk, 2 * images, DC), BF),
            pltpu.VMEM((nch, 5, block, DC), BF),
            pltpu.VMEM((2 * nch, 4 * block, DC), F32),
            pltpu.VMEM((4 * block, 2 * hid), BF),
            pltpu.VMEM((nch, 4, block, DC), BF),
            pltpu.VMEM((nch, 4, block, DC), BF),
            pltpu.VMEM((nch, nk, 2 * images, DC), BF),
            dma((images,)),
            dma((2,)),
            dma((3,)),
            dma((3,)),
            dma,
            dma((nch,)),
            dma,
            dma((nch,)),
            dma,
            dma((nch,)),
            dma,
            dma((nch,)),
        ],
        compiler_params=pltpu.CompilerParams(
            collective_id=0, has_side_effects=True, vmem_limit_bytes=60 * 1024 * 1024
        ),
        name="exchange",
    )(tokens, slot_keys, logit_scale, up_weight, up_bias, down_weight, down_bias)
    return pl.pallas_call(
        functools.partial(mix_kernel, nch),
        grid=(images,),
        out_shape=jax.ShapeDtypeStruct(tokens.shape, BF),
        in_specs=[
            pl.BlockSpec((patches, cols), lambda i: (i, 0)),
            pl.BlockSpec((nch, nk, 2 * images, DC), lambda i: (0, 0, 0, 0)),
        ],
        out_specs=pl.BlockSpec((1, patches, width), lambda i: (i, 0, 0)),
        name="mix",
    )(comb, got)


def solution(mesh):
    return jax.shard_map(
        body,
        mesh=mesh,
        in_specs=(
            P(("dp", "expert"), None, None),
            P(),
            P(),
            P("expert", None, "dp"),
            P("expert", "dp"),
            P("expert", "dp", None),
            P(),
        ),
        out_specs=P(("dp", "expert"), None, None),
        check_vma=False,
    )
```

time: 184 us -> 72.7 us (0.40)
  waiting for transfers between devices: 84 us -> 0 us
  Pallas kernels: 0 us -> 69.8 us
  blocking collectives: 32.5 us -> 0 us
  matrix products: 29.8 us -> 0 us
  starting transfers between devices: 16.4 us -> 0 us
  other arithmetic: 10.3 us -> 0 us
  local copies, waits for them, and re-layouts: 9.2 us -> 1.81 us
    all_to_all x3 -> x0, waiting for transfers between devices: 84 us -> none  [the longest x1 32.6 us: sent_to_all(): lax.all_to_all(jnp.broadcast_to(x[None], (count, *x.shape)), axis, 0, 0,...]
    pallas_call x0 -> x2, Pallas kernels: none -> 69.8 us  [the longest x1 65.3 us: body(): pl.pallas_call(functools.partial(exchange_kernel, nk, nch), out_shape=(ja...]
    all_to_all x1 -> x0, blocking collectives: 32.5 us -> none  [body(): lax.all_to_all(slot_inputs, 'expert', split_axis=1, concat_axis=0, tiled=...]
    dot_general x4 -> x0, matrix products: 29.8 us -> none  [the longest x1 20.2 us: body(): jnp.einsum('rkf,kfd->rkd', hidden, down_weight, preferred_element_type=jn...]
    all_to_all x3 -> x0, starting transfers between devices: 16.4 us -> none  [the longest x1 7.04 us: body(): lax.all_to_all(finished, 'expert', split_axis=0, concat_axis=0, tiled=True)]
    reduce_sum x3 -> x0, other arithmetic: 6.82 us -> none  [the longest x2 3.53 us: unit_rms(): jnp.mean(values * values, axis=axis_pos, keepdims=True) + norm_eps]
    broadcast_in_dim x2 -> x0, local copies, waits for them, and re-layouts: 4.97 us -> none  [sent_to_all(): jnp.broadcast_to(x[None], (count, *x.shape))]
    convert_element_type x2 -> x0, other arithmetic: 3.13 us -> none  [the longest x1 2.38 us: body(): (summed + own_bias[None]).astype(jnp.bfloat16)]
  transfers between devices with their start and end apart: 3 -> 0, of which waited for: 3 -> 0; matrix products, arithmetic and copies ran while one was open for 0% -> 0% of each run, Pallas kernels for 0% -> 0%
where the time goes in v1:
time: 72.7 us; the launch traced here: 72.3 us
  Pallas kernels  69.8 us (96%)
  local copies, waits for them, and re-layouts  1.81 us (2%)
    pallas_call x1, Pallas kernels, body(): pl.pallas_call(functools.partial(exchange_kernel, nk, nch), out_shape=(ja...  65.3 us
    pallas_call x1, Pallas kernels, body(): pl.pallas_call(functools.partial(mix_kernel, nch), grid=(images,), out_sh...  4.45 us
    unnamed x1, local copies, waits for them, and re-layouts  1.81 us

profile of v1, /device:TPU:8, one launch (start us, length us, event | category | flops | bytes accessed | tf_op | source)
XLA Modules:
  0.0 72.3 jit_solution(5999471335085880647)
XLA Ops:
  0.7 1.8 %copy.8.keys_ref = bf16[1280,64]{1,0:T(8,128)(2,1)} copy(bf16[1280,64]{0,1:T(8,128)(2,1)} %param.8) | data formatting | bytes 327680 | tf_op args[1]
  2.5 65.3 %exchange.1 = (bf16[1024,256]{1,0:T(8,128)(2,1)}, bf16[5,32,8,256]{3,2,1,0:T(8,128)(2,1)}) custom-call(bf16[4,256,1280]{2,1,0:T(8,128)(2,1)} %tok_hbm.1, bf16[1280,64]{1,0:T(8,128)(2,1)} %copy.8.keys_ref, f32[1]{0:T(128)S(6)} %copy.9.scale_ref, bf16[1,1280,1280]{2,1,0:T(8,128)(2,1)} %up_hbm.1, bf16[1,1280]{1,0:T(2,128)(2,1)} %upb_ref.1, ...), custom_call_target="tpu_custom_call" | custom-call | tf_op jit(solution)/shard_map/exchange/pallas_call | solution.py:325
  67.8 4.5 %mix.1 = bf16[4,256,1280]{2,1,0:T(8,128)(2,1)} custom-call(bf16[1024,256]{1,0:T(8,128)(2,1)} %get-tuple-element.7.comb_ref, bf16[5,32,8,256]{3,2,1,0:T(8,128)(2,1)} %get-tuple-element.8.got_ref), custom_call_target="tpu_custom_call" | custom-call | tf_op jit(solution)/shard_map/mix/pallas_call | solution.py:369

commit v2 on v1

v2 whole, which is shorter than its diff:
```python
import functools

import jax
import jax.numpy as jnp
from jax import lax
from jax.experimental import pallas as pl
from jax.experimental.pallas import tpu as pltpu
from jax.sharding import PartitionSpec as P

norm_eps = 1e-06
MESH = pl.DeviceIdType.MESH
DC = 256
BF = jnp.bfloat16
F32 = jnp.float32


def iota(shape, dim):
    return lax.broadcasted_iota(jnp.int32, shape, dim)


def dot(a, b):
    return jnp.dot(a, b, preferred_element_type=F32)


def exchange_kernel(
    nk,
    nch,
    tok_hbm,
    keys_hbm,
    scale_hbm,
    up_hbm,
    upb_hbm,
    down_hbm,
    downb_hbm,
    out_ref,
    tok,
    keys_ref,
    scale_ref,
    upb_ref,
    downb_ref,
    disp_t,
    keyrep,
    scores,
    perm,
    permt,
    wup,
    wdown,
    bup,
    bias_rows,
    slots_s,
    slots_r,
    rows,
    pre,
    hidden,
    part_s,
    part_r,
    fin,
    comb,
    got,
    tok_sem,
    load_sem,
    wsend_sem,
    wrecv_sem,
    s1_sem,
    r1_sem,
    s2_sem,
    r2_sem,
    s3_sem,
    r3_sem,
    s4_sem,
    r4_sem,
):
    images, patches, width = tok.shape
    block = images * nk
    own = lax.axis_index("expert")
    dp = lax.axis_index("dp")
    k_own = lax.div(own, 2)
    parity = lax.rem(own, 2)
    flip = own + 1 - 2 * parity
    far = lax.rem(dp + 2, 4)
    core = dp + 1 - 2 * lax.rem(dp, 2)
    members = ((dp, own), (dp, flip), (far, flip), (far, own))

    def peer(step):
        k = lax.rem(k_own + step, nk)
        return k, {"dp": dp, "expert": 2 * k + parity}

    tok_in = [
        pltpu.make_async_copy(tok_hbm.at[i], tok.at[i], tok_sem.at[i]) for i in range(images)
    ]
    keys_in = pltpu.make_async_copy(keys_hbm, keys_ref, load_sem.at[2])
    scale_in = pltpu.make_async_copy(scale_hbm, scale_ref, load_sem.at[3])
    upb_in = pltpu.make_async_copy(upb_hbm, upb_ref, load_sem.at[4])
    downb_in = pltpu.make_async_copy(downb_hbm, downb_ref, load_sem.at[5])
    for copy in (keys_in, scale_in, *tok_in, upb_in, downb_in):
        copy.start()
    up_in = pltpu.make_async_copy(up_hbm.at[0], wup.at[0], load_sem.at[0])
    down_in = pltpu.make_async_copy(down_hbm.at[0], wdown.at[0], load_sem.at[1])
    up_in.start()
    down_in.start()

    barrier = pltpu.get_barrier_semaphore()

    def greet(step, _):
        _, where = peer(step)
        pl.semaphore_signal(barrier, inc=1, device_id=where, device_id_type=MESH)
        return 0

    lax.fori_loop(1, nk, greet, 0)
    for d, e in members[1:]:
        pl.semaphore_signal(barrier, inc=1, device_id={"dp": d, "expert": e}, device_id_type=MESH)
    pl.semaphore_signal(barrier, inc=1, device_id={"dp": core, "expert": own}, device_id_type=MESH)

    keys_in.wait()
    keys = keys_ref[...].astype(F32)
    keys = keys * lax.rsqrt(jnp.mean(keys * keys, axis=1, keepdims=True) + norm_eps)
    n_exp = keys.shape[0]
    spread = lax.div(iota((n_exp * images, n_exp), 0), images) == iota((n_exp * images, n_exp), 1)
    keyrep[...] = jnp.transpose(dot(spread.astype(BF), keys.astype(BF))).astype(BF)

    scale_in.wait()
    scale = scale_ref[0]
    for i in range(images):
        tok_in[i].wait()
        t = tok[i]
        tf = t.astype(F32)
        factor = lax.rsqrt(jnp.mean(tf * tf, axis=1, keepdims=True) + norm_eps)
        logits = scale * (dot(t, keyrep[...]) * factor) / width
        scores[pl.ds(i * patches, patches), :] = logits
        mask = lax.rem(iota(logits.shape, 1), images) == i
        e_tok = jnp.exp(logits - jnp.max(logits, axis=0, keepdims=True))
        share = e_tok / jnp.sum(e_tok, axis=0, keepdims=True)
        share = jnp.where(mask, share, 0.0)
        disp_t[:, pl.ds(i * patches, patches)] = jnp.transpose(share).astype(BF)

    pl.semaphore_wait(barrier, nk - 1 + 4)

    where_core = {"dp": core, "expert": own}
    sends_w = []
    for j, (src_ref, dst_ref) in enumerate(
        ((up_hbm.at[0], wup.at[1]), (down_hbm.at[0], wdown.at[1]), (upb_hbm, bup))
    ):
        sends_w.append(
            pltpu.make_async_remote_copy(
                src_ref=src_ref,
                dst_ref=dst_ref,
                send_sem=wsend_sem.at[j],
                recv_sem=wrecv_sem.at[j],
                device_id=where_core,
                device_id_type=MESH,
            )
        )

    def lanes(c):
        return pl.ds(pl.multiple_of(c * DC, DC), DC)

    def send_tiles(buf, dst, c, s_sem, r_sem):
        def one(step, _):
            k, where = peer(step)
            pltpu.make_async_remote_copy(
                src_ref=buf.at[c, k],
                dst_ref=dst.at[c, k_own],
                send_sem=s_sem,
                recv_sem=r_sem.at[c],
                device_id=where,
                device_id_type=MESH,
            ).start()
            return 0

        lax.fori_loop(1, nk, one, 0)

    def dispatch(c, _):
        t = tok[:, :, lanes(c)].reshape(images * patches, DC)
        s = dot(disp_t[...], t)
        slots_s[c] = s.reshape(nk, 2 * images, DC).astype(BF)
        slots_r[c, k_own] = slots_s[c, k_own]
        send_tiles(slots_s, slots_r, c, s1_sem, r1_sem)
        return 0

    for copy in sends_w:
        copy.start()
    lax.fori_loop(0, nch, dispatch, 0)

    row = iota(perm.shape, 0)
    col = iota(perm.shape, 1)
    rel = lax.rem(lax.div(row, block) + parity, 2)
    within = lax.rem(row, block)
    src = lax.div(within, images) * (2 * images) + rel * images + lax.rem(within, images)
    perm[...] = (src == col).astype(BF)
    row_t = iota(perm.shape, 1)
    col_t = iota(perm.shape, 0)
    rel_t = lax.rem(lax.div(row_t, block) + parity, 2)
    within_t = lax.rem(row_t, block)
    src_t = lax.div(within_t, images) * (2 * images) + rel_t * images + lax.rem(within_t, images)
    permt[...] = (src_t == col_t).astype(BF)

    downb_in.wait()
    n_row = 2 * k_own + lax.rem(lax.div(iota((2 * block, n_exp), 0), block) + parity, 2)
    pick = (n_row == iota((2 * block, n_exp), 1)).astype(BF)
    for c in range(nch):
        bias_rows[c] = dot(pick, downb_ref[:, c * DC : (c + 1) * DC]).astype(BF)

    def mix_weights(i, _):
        tokens_of = pl.ds(pl.multiple_of(i * patches, patches), patches)
        logits = scores[tokens_of, :]
        mask = lax.rem(iota(logits.shape, 1), images) == i
        e_slot = jnp.where(mask, jnp.exp(logits - jnp.max(logits, axis=1, keepdims=True)), 0.0)
        mix = e_slot / jnp.sum(e_slot, axis=1, keepdims=True)
        comb[tokens_of, :] = mix.astype(BF)
        return 0

    lax.fori_loop(0, images, mix_weights, 0)

    def to_member(src_ref, dst_ref, c, m, s_sem, r_sem):
        d, e = members[m]
        return pltpu.make_async_remote_copy(
            src_ref=src_ref,
            dst_ref=dst_ref.at[c, m],
            send_sem=s_sem,
            recv_sem=r_sem.at[c],
            device_id={"dp": d, "expert": e},
            device_id_type=MESH,
        )

    def wait_tiles(buf, c, r_sem):
        pltpu.make_async_copy(
            buf.at[c, pl.ds(0, nk - 1)], buf.at[c, pl.ds(0, nk - 1)], r_sem.at[c]
        ).wait()

    def wait_members(buf, c, r_sem):
        pltpu.make_async_copy(
            buf.at[c, pl.ds(1, 3)], buf.at[c, pl.ds(1, 3)], r_sem.at[c]
        ).wait()

    def spread_x(c, _):
        wait_tiles(slots_r, c, r1_sem)
        got = slots_r[c].reshape(2 * block, DC)
        moved = dot(perm[...], got).astype(BF)
        rows[c, 0] = moved[:block]
        rows[c, 4] = moved[block:]
        for m, piece in ((3, 0), (1, 4), (2, 4)):
            to_member(rows.at[c, piece], rows, c, m, s2_sem, r2_sem).start()
        return 0

    def up(c, first):
        wait_members(rows, c, r2_sem)
        x = rows[c, pl.ds(0, 4)].reshape(4 * block, DC)

        for j in range(2 * nch):
            half, at = divmod(j, nch)
            part = dot(x, wup[half, lanes(c), at * DC : (at + 1) * DC])
            pre[j] = part if first else pre[j] + part
        return 0

    spread_x(0, 0)
    up_in.wait()
    sends_w[0].wait_recv()
    spread_x(1, 0)
    up(0, True)

    def spread_and_up(c, _):
        spread_x(c, 0)
        up(c - 1, False)
        return 0

    lax.fori_loop(2, nch, spread_and_up, 0)
    up(nch - 1, False)

    sends_w[2].wait_recv()

    def activate(half, bias_ref):
        def one(j, _):
            v = pre[half * nch + j] + bias_ref[:, lanes(j)].astype(F32)
            h = 0.5 * v * (1.0 + lax.erf(v * (2.0**-0.5)))
            hidden[:, lanes(half * nch + j)] = h.astype(BF)
            return 0

        lax.fori_loop(0, nch, one, 0)

    upb_in.wait()
    activate(0, upb_ref)
    activate(1, bup)
    down_in.wait()
    sends_w[1].wait_recv()

    def down(c, _):
        p = dot(hidden[:, pl.ds(0, width)], wdown[0, :, lanes(c)])
        p = p + dot(hidden[:, pl.ds(width, width)], wdown[1, :, lanes(c)])
        part_s[c] = p.astype(BF).reshape(4, block, DC)
        for m in (3, 1, 2):
            to_member(part_s.at[c, m], part_r, c, m, s3_sem, r3_sem).start()
        return 0

    lax.fori_loop(0, nch, down, 0)

    def finish(c, _):
        wait_members(part_r, c, r3_sem)
        mine = part_s[c, 0].astype(F32) + part_r[c, 3].astype(F32)
        other = part_r[c, 1].astype(F32) + part_r[c, 2].astype(F32)
        total = jnp.concatenate([mine, other], axis=0) + bias_rows[c].astype(F32)
        moved = dot(permt[...], total.astype(BF))
        fin[c] = moved.reshape(nk, 2 * images, DC).astype(BF)
        got[c, k_own] = fin[c, k_own]
        send_tiles(fin, got, c, s4_sem, r4_sem)
        return 0

    lax.fori_loop(0, nch, finish, 0)

    def arrive(c, _):
        wait_tiles(got, c, r4_sem)
        back = got[c].reshape(2 * block, DC)
        for i in range(images):
            mixed = dot(comb[pl.ds(i * patches, patches), :], back)
            out_ref[i, :, lanes(c)] = mixed.astype(BF)
        return 0

    lax.fori_loop(0, nch, arrive, 0)

    def drain(buf, first, count, sem):
        view = buf.at[:, pl.ds(first, count)]
        pltpu.make_async_copy(view, view, sem).wait()

    for copy in sends_w:
        copy.wait_send()
    drain(slots_s, 0, nk - 1, s1_sem)
    drain(rows, 1, 3, s2_sem)
    drain(part_s, 1, 3, s3_sem)
    drain(fin, 0, nk - 1, s4_sem)


def body(tokens, slot_keys, logit_scale, up_weight, up_bias, down_weight, down_bias):
    images, patches, width = tokens.shape
    nk = lax.axis_size("expert") // 2
    nch = width // DC
    n_exp = 2 * nk
    cols = n_exp * images
    block = images * nk
    hid = up_weight.shape[2]
    dma = pltpu.SemaphoreType.DMA
    vmem = pl.BlockSpec(memory_space=pltpu.VMEM)
    hbm = pl.BlockSpec(memory_space=pltpu.HBM)
    return pl.pallas_call(
        functools.partial(exchange_kernel, nk, nch),
        out_shape=pltpu.VMEM(tokens.shape, BF),
        in_specs=[hbm] * 7,
        out_specs=vmem,
        scratch_shapes=[
            pltpu.VMEM((images, patches, width), BF),
            pltpu.VMEM((n_exp, width), BF),
            pltpu.SMEM((1,), F32),
            pltpu.VMEM((1, hid), BF),
            pltpu.VMEM((n_exp, width), BF),
            pltpu.VMEM((cols, images * patches), BF),
            pltpu.VMEM((width, cols), BF),
            pltpu.VMEM((images * patches, cols), F32),
            pltpu.VMEM((2 * block, 2 * block), BF),
            pltpu.VMEM((2 * block, 2 * block), BF),
            pltpu.VMEM((2, width, hid), BF),
            pltpu.VMEM((2, hid, width), BF),
            pltpu.VMEM((1, hid), BF),
            pltpu.VMEM((nch, 2 * block, DC), BF),
            pltpu.VMEM((nch, nk, 2 * images, DC), BF),
            pltpu.VMEM((nch, nk, 2 * images, DC), BF),
            pltpu.VMEM((nch, 5, block, DC), BF),
            pltpu.VMEM((2 * nch, 4 * block, DC), F32),
            pltpu.VMEM((4 * block, 2 * hid), BF),
            pltpu.VMEM((nch, 4, block, DC), BF),
            pltpu.VMEM((nch, 4, block, DC), BF),
            pltpu.VMEM((nch, nk, 2 * images, DC), BF),
            pltpu.VMEM((images * patches, cols), BF),
            pltpu.VMEM((nch, nk, 2 * images, DC), BF),
            dma((images,)),
            dma((6,)),
            dma((3,)),
            dma((3,)),
            dma,
            dma((nch,)),
            dma,
            dma((nch,)),
            dma,
            dma((nch,)),
            dma,
            dma((nch,)),
        ],
        compiler_params=pltpu.CompilerParams(
            collective_id=0, has_side_effects=True, vmem_limit_bytes=58 * 1024 * 1024
        ),
        name="exchange",
    )(tokens, slot_keys.T, logit_scale, up_weight, up_bias, down_weight, down_bias)


def solution(mesh):
    return jax.shard_map(
        body,
        mesh=mesh,
        in_specs=(
            P(("dp", "expert"), None, None),
            P(),
            P(),
            P("expert", None, "dp"),
            P("expert", "dp"),
            P("expert", "dp", None),
            P(),
        ),
        out_specs=P(("dp", "expert"), None, None),
        check_vma=False,
    )
```

time: 72.7 us -> 63 us (0.87)
  Pallas kernels: 69.8 us -> 60.8 us
    pallas_call x2 -> x1, Pallas kernels: 69.8 us -> 60.8 us  [body(): pl.pallas_call(functools.partial(exchange_kernel, nk, nch), out_shape=plt...]
where the time goes in v2:
time: 63 us; the launch traced here: 62.9 us
  Pallas kernels  60.8 us (97%)
  local copies, waits for them, and re-layouts  1.49 us (2%)
  between operations  0.66 us (1%)
    pallas_call x1, Pallas kernels, body(): pl.pallas_call(functools.partial(exchange_kernel, nk, nch), out_shape=plt...  60.8 us
    unnamed x1, local copies, waits for them, and re-layouts  1.49 us

profile of v2, /device:TPU:8, one launch (start us, length us, event | category | flops | bytes accessed | tf_op | source)
XLA Modules:
  0.0 62.9 jit_solution(7988543615442936880)
XLA Ops:
  0.7 60.8 %exchange.1 = bf16[4,256,1280]{2,1,0:T(8,128)(2,1)S(1)} custom-call(bf16[4,256,1280]{2,1,0:T(8,128)(2,1)} %tok_hbm.1, bf16[64,1280]{1,0:T(8,128)(2,1)} %bitcast.1, f32[1]{0:T(128)S(6)} %copy.10.scale_hbm, bf16[1,1280,1280]{2,1,0:T(8,128)(2,1)} %up_hbm.1, bf16[1,1280]{1,0:T(2,128)(2,1)} %upb_hbm.1, bf16[1,1280,1280]{2,1,0:T(8,128)(2,1)} %down_hbm.1, ...), custom_call_target="tpu_custom_call" | custom-call | tf_op jit(solution)/shard_map/exchange/pallas_call | solution.py:342
  61.4 1.5 %copy.9 = bf16[4,256,1280]{2,1,0:T(8,128)(2,1)} copy(bf16[4,256,1280]{2,1,0:T(8,128)(2,1)S(1)} %exchange.1) | data formatting | bytes 5242880

commit v3 on v2

v3 whole, which is shorter than its diff:
```python
import functools

import jax
import jax.numpy as jnp
from jax import lax
from jax.experimental import pallas as pl
from jax.experimental.pallas import tpu as pltpu
from jax.sharding import PartitionSpec as P

norm_eps = 1e-06
MESH = pl.DeviceIdType.MESH
LN = 128
DC = 2 * LN
HALVES = 2
BF = jnp.bfloat16
F32 = jnp.float32


def iota(shape, dim):
    return lax.broadcasted_iota(jnp.int32, shape, dim)


def dot(a, b):
    return jnp.dot(a, b, preferred_element_type=F32)


def exchange_kernel(
    nk,
    nch,
    tok_hbm,
    keys_hbm,
    scale_hbm,
    up_hbm,
    upb_hbm,
    down_hbm,
    downb_hbm,
    out_ref,
    tok,
    keys_ref,
    scale_ref,
    upb_ref,
    downb_ref,
    disp_t,
    keyrep,
    scores,
    perm,
    permt,
    wup,
    wdown,
    bup,
    bias_rows,
    slots_s,
    slots_r,
    rows,
    pre,
    hidden,
    part_s,
    part_r,
    fin,
    comb,
    got,
    tok_sem,
    load_sem,
    wsend_sem,
    wrecv_sem,
    s1_sem,
    r1_sem,
    s2_sem,
    r2_sem,
    s3_sem,
    r3_sem,
    s4_sem,
    r4_sem,
):
    images, patches, width = tok.shape
    ih = images // HALVES
    tile = 4 * ih
    sub = nk * ih
    block = 2 * sub
    n_exp = keys_ref.shape[0]
    units = HALVES * nch
    own = lax.axis_index("expert")
    dp = lax.axis_index("dp")
    k_own = lax.div(own, 2)
    parity = lax.rem(own, 2)
    flip = own + 1 - 2 * parity
    far = lax.rem(dp + 2, 4)
    core = dp + 1 - 2 * lax.rem(dp, 2)
    members = ((dp, own), (dp, flip), (far, flip), (far, own))

    def peer(step):
        k = lax.rem(k_own + step, nk)
        return k, {"dp": dp, "expert": 2 * k + parity}

    tok_in = [
        pltpu.make_async_copy(tok_hbm.at[i], tok.at[i], tok_sem.at[i]) for i in range(images)
    ]
    keys_in = pltpu.make_async_copy(keys_hbm, keys_ref, load_sem.at[2])
    scale_in = pltpu.make_async_copy(scale_hbm, scale_ref, load_sem.at[3])
    upb_in = pltpu.make_async_copy(upb_hbm, upb_ref, load_sem.at[4])
    downb_in = pltpu.make_async_copy(downb_hbm, downb_ref, load_sem.at[5])
    for copy in (keys_in, scale_in, *tok_in, upb_in, downb_in):
        copy.start()
    up_in = pltpu.make_async_copy(up_hbm.at[0], wup.at[0], load_sem.at[0])
    down_in = pltpu.make_async_copy(down_hbm.at[0], wdown.at[0], load_sem.at[1])
    up_in.start()
    down_in.start()

    barrier = pltpu.get_barrier_semaphore()

    def greet(step, _):
        _, where = peer(step)
        pl.semaphore_signal(barrier, inc=1, device_id=where, device_id_type=MESH)
        return 0

    for step in range(1, nk):
        greet(step, 0)
    for d, e in members[1:]:
        pl.semaphore_signal(barrier, inc=1, device_id={"dp": d, "expert": e}, device_id_type=MESH)
    pl.semaphore_signal(barrier, inc=1, device_id={"dp": core, "expert": own}, device_id_type=MESH)

    keys_in.wait()
    keys = keys_ref[...].astype(F32)
    keys = keys * lax.rsqrt(jnp.mean(keys * keys, axis=1, keepdims=True) + norm_eps)
    col = iota((nk * tile, n_exp), 0)
    col = 2 * lax.div(col, tile) + lax.rem(lax.div(col, ih), 2)
    spread = (col == iota((nk * tile, n_exp), 1)).astype(BF)
    keyrep[...] = jnp.transpose(dot(spread, keys.astype(BF))).astype(BF)

    def place_mask(shape, dim, i, cc):
        at = iota(shape, dim)
        return (lax.rem(at, ih) == i) & (lax.rem(lax.div(at, 2 * ih), 2) == cc)

    scale_in.wait()
    scale = scale_ref[0]

    def soften(images_of):
        for i in images_of:
            tok_in[i].wait()
            t = tok[i]
            tf = t.astype(F32)
            factor = lax.rsqrt(jnp.mean(tf * tf, axis=1, keepdims=True) + norm_eps)
            logits = scale * (dot(t, keyrep[...]) * factor) / width
            scores[pl.ds(i * patches, patches), :] = logits
            e_tok = jnp.exp(logits - jnp.max(logits, axis=0, keepdims=True))
            share = jnp.transpose(e_tok / jnp.sum(e_tok, axis=0, keepdims=True))
            half, at = divmod(i, ih)
            for cc in range(2):
                kept = jnp.where(place_mask(share.shape, 0, at, cc), share, 0.0)
                disp_t[half, cc, :, pl.ds(at * patches, patches)] = kept.astype(BF)

    soften(range(ih))

    pl.semaphore_wait(barrier, nk - 1 + 4)

    where_core = {"dp": core, "expert": own}
    sends_w = []
    for j, (src_ref, dst_ref) in enumerate(
        ((up_hbm.at[0], wup.at[1]), (down_hbm.at[0], wdown.at[1]), (upb_hbm, bup))
    ):
        sends_w.append(
            pltpu.make_async_remote_copy(
                src_ref=src_ref,
                dst_ref=dst_ref,
                send_sem=wsend_sem.at[j],
                recv_sem=wrecv_sem.at[j],
                device_id=where_core,
                device_id_type=MESH,
            )
        )

    def lanes(c):
        return pl.ds(pl.multiple_of(c * DC, DC), DC)

    def lane_tile(c, cc):
        return pl.ds(pl.multiple_of(c * DC + cc * LN, LN), LN)

    def of(u):
        half = lax.div(u, nch)
        return half, u - half * nch

    def send_tiles(buf, dst, u, s_sem, r_sem):
        def one(step, _):
            k, where = peer(step)
            pltpu.make_async_remote_copy(
                src_ref=buf.at[u, k],
                dst_ref=dst.at[u, k_own],
                send_sem=s_sem,
                recv_sem=r_sem.at[u],
                device_id=where,
                device_id_type=MESH,
            ).start()
            return 0

        for step in range(1, nk):
            one(step, 0)

    def dispatch(u):
        half, c = of(u)
        ts = tok[pl.ds(half * ih, ih), :, lanes(c)].reshape(ih * patches, DC)
        s = dot(disp_t[half, 0], ts[:, :LN]) + dot(disp_t[half, 1], ts[:, LN:])
        slots_s[u] = s.reshape(nk, tile, LN).astype(BF)
        slots_r[u, k_own] = slots_s[u, k_own]
        send_tiles(slots_s, slots_r, u, s1_sem, r1_sem)

    def to_member(src_ref, dst_ref, u, m, s_sem, r_sem):
        d, e = members[m]
        return pltpu.make_async_remote_copy(
            src_ref=src_ref,
            dst_ref=dst_ref.at[u, m],
            send_sem=s_sem,
            recv_sem=r_sem.at[u],
            device_id={"dp": d, "expert": e},
            device_id_type=MESH,
        )

    def wait_tiles(buf, u, r_sem):
        view = buf.at[u, pl.ds(0, nk - 1)]
        pltpu.make_async_copy(view, view, r_sem.at[u]).wait()

    def wait_members(buf, u, r_sem):
        view = buf.at[u, pl.ds(1, 3)]
        pltpu.make_async_copy(view, view, r_sem.at[u]).wait()

    def spread_x(u):
        wait_tiles(slots_r, u, r1_sem)
        moved = dot(perm[...], slots_r[u].reshape(2 * block, LN)).astype(BF)
        rows[u, 0] = moved[:block]
        rows[u, 4] = moved[block:]
        for m, piece in ((3, 0), (1, 4), (2, 4)):
            to_member(rows.at[u, piece], rows, u, m, s2_sem, r2_sem).start()

    def up(u):
        half, c = of(u)
        wait_members(rows, u, r2_sem)
        x = jnp.concatenate(
            [rows[u, pl.ds(0, 4), pl.ds(0, sub)], rows[u, pl.ds(0, 4), pl.ds(sub, sub)]], axis=2
        ).reshape(4 * sub, DC)
        for j in range(2 * nch):
            which, at = divmod(j, nch)
            pre[half, j] += dot(x, wup[which, lanes(c), at * DC : (at + 1) * DC])

    def activate(half):
        for which, bias_ref in ((0, upb_ref), (1, bup)):

            def one(j, _, which=which, bias_ref=bias_ref):
                v = pre[half, which * nch + j] + bias_ref[:, lanes(j)].astype(F32)
                h = 0.5 * v * (1.0 + lax.erf(v * (2.0**-0.5)))
                hidden[half, :, lanes(which * nch + j)] = h.astype(BF)
                return 0

            lax.fori_loop(0, nch, one, 0)

    def down(u):
        half, c = of(u)
        p = dot(hidden[half, :, pl.ds(0, width)], wdown[0, :, lanes(c)])
        p = p + dot(hidden[half, :, pl.ds(width, width)], wdown[1, :, lanes(c)])
        p = p.astype(BF)
        part_s[u, :, pl.ds(0, sub)] = p[:, :LN].reshape(4, sub, LN)
        part_s[u, :, pl.ds(sub, sub)] = p[:, LN:].reshape(4, sub, LN)
        for m in (3, 1, 2):
            to_member(part_s.at[u, m], part_r, u, m, s3_sem, r3_sem).start()

    def finish(u):
        half, c = of(u)
        wait_members(part_r, u, r3_sem)
        mine = part_s[u, 0].astype(F32) + part_r[u, 3].astype(F32)
        other = part_r[u, 1].astype(F32) + part_r[u, 2].astype(F32)
        total = jnp.concatenate([mine, other], axis=0) + bias_rows[c].astype(F32)
        moved = dot(permt[...], total.astype(BF))
        fin[u] = moved.reshape(nk, tile, LN).astype(BF)
        got[u, k_own] = fin[u, k_own]
        send_tiles(fin, got, u, s4_sem, r4_sem)

    def mix(u):
        half, c = of(u)
        wait_tiles(got, u, r4_sem)
        back = got[u].reshape(2 * block, LN)
        for at in range(ih):
            for cc in range(2):
                mixed = dot(comb[half, cc, pl.ds(at * patches, patches), :], back)
                out_ref[half * ih + at, :, lane_tile(c, cc)] = mixed.astype(BF)

    def mix_weights(i, _):
        logits = scores[pl.ds(pl.multiple_of(i * patches, patches), patches), :]
        half = lax.div(i, ih)
        at = lax.rem(i, ih)
        masks = [place_mask(logits.shape, 1, at, cc) for cc in range(2)]
        e_slot = jnp.exp(logits - jnp.max(logits, axis=1, keepdims=True))
        total = jnp.sum(jnp.where(masks[0], e_slot, 0.0), axis=1, keepdims=True)
        share = e_slot / total
        for cc in range(2):
            kept = jnp.where(masks[cc], share, 0.0)
            comb[half, cc, pl.ds(pl.multiple_of(at * patches, patches), patches), :] = kept.astype(BF)
        return 0

    def prepare():
        def source(shape, dim):
            row = iota(shape, dim)
            e = lax.rem(lax.div(row, block) + parity, 2)
            cc = lax.rem(lax.div(row, sub), 2)
            within = lax.rem(row, sub)
            return lax.div(within, ih) * tile + cc * 2 * ih + e * ih + lax.rem(within, ih)

        perm[...] = (source(perm.shape, 0) == iota(perm.shape, 1)).astype(BF)
        permt[...] = (source(perm.shape, 1) == iota(perm.shape, 0)).astype(BF)
        for half in range(HALVES):
            for j in range(2 * nch):
                pre[half, j] = jnp.zeros((4 * sub, DC), F32)

    def prepare_later():
        lax.fori_loop(0, images, mix_weights, 0)
        downb_in.wait()
        shape = (2 * block, n_exp)
        n_row = 2 * k_own + lax.rem(lax.div(iota(shape, 0), block) + parity, 2)
        pick = (n_row == iota(shape, 1)).astype(BF)
        first = lax.rem(lax.div(iota((2 * block, LN), 0), sub), 2) == 0
        for c in range(nch):
            both = dot(pick, downb_ref[:, c * DC : (c + 1) * DC])
            bias_rows[c] = jnp.where(first, both[:, :LN], both[:, LN:]).astype(BF)

    def run(first, last, *steps):
        def one(t, _):
            for step, shift in steps:
                step(t + shift)
            return 0

        lax.fori_loop(first, last, one, 0)

    ahead = units - 3
    sends_w[2].start()
    run(0, nch, (dispatch, 0))
    soften(range(ih, images))
    run(nch, ahead, (dispatch, 0))
    sends_w[0].start()
    sends_w[1].start()
    prepare()
    prepare_later()
    run(0, 3, (spread_x, 0), (dispatch, ahead))
    up_in.wait()
    sends_w[0].wait_recv()
    run(0, nch, (spread_x, 3), (up, 0))
    upb_in.wait()
    sends_w[2].wait_recv()
    spread_x(nch + 3)
    activate(0)
    spread_x(nch + 4)
    down_in.wait()
    sends_w[1].wait_recv()
    run(0, nch, (down, 0))

    run(0, nch, (up, nch))
    activate(1)
    run(0, nch, (down, nch), (finish, 0))
    run(0, nch, (finish, nch), (mix, 0))
    run(nch, units, (mix, 0))

    def drain(buf, first, count, sem):
        view = buf.at[:, pl.ds(first, count)]
        pltpu.make_async_copy(view, view, sem).wait()

    for copy in sends_w:
        copy.wait_send()
    drain(slots_s, 0, nk - 1, s1_sem)
    drain(rows, 1, 3, s2_sem)
    drain(part_s, 1, 3, s3_sem)
    drain(fin, 0, nk - 1, s4_sem)


def body(tokens, slot_keys, logit_scale, up_weight, up_bias, down_weight, down_bias):
    images, patches, width = tokens.shape
    nk = lax.axis_size("expert") // 2
    nch = width // DC
    n_exp = 2 * nk
    ih = images // HALVES
    tile = 4 * ih
    cols = nk * tile
    sub = nk * ih
    units = HALVES * nch
    hid = up_weight.shape[2]
    dma = pltpu.SemaphoreType.DMA
    vmem = pl.BlockSpec(memory_space=pltpu.VMEM)
    hbm = pl.BlockSpec(memory_space=pltpu.HBM)
    return pl.pallas_call(
        functools.partial(exchange_kernel, nk, nch),
        out_shape=pltpu.VMEM(tokens.shape, BF),
        in_specs=[hbm] * 7,
        out_specs=vmem,
        scratch_shapes=[
            pltpu.VMEM((images, patches, width), BF),
            pltpu.VMEM((n_exp, width), BF),
            pltpu.SMEM((1,), F32),
            pltpu.VMEM((1, hid), BF),
            pltpu.VMEM((n_exp, width), BF),
            pltpu.VMEM((HALVES, 2, cols, ih * patches), BF),
            pltpu.VMEM((width, cols), BF),
            pltpu.VMEM((images * patches, cols), F32),
            pltpu.VMEM((4 * sub, 4 * sub), BF),
            pltpu.VMEM((4 * sub, 4 * sub), BF),
            pltpu.VMEM((2, width, hid), BF),
            pltpu.VMEM((2, hid, width), BF),
            pltpu.VMEM((1, hid), BF),
            pltpu.VMEM((nch, 4 * sub, LN), BF),
            pltpu.VMEM((units, nk, tile, LN), BF),
            pltpu.VMEM((units, nk, tile, LN), BF),
            pltpu.VMEM((units, 5, 2 * sub, LN), BF),
            pltpu.VMEM((HALVES, 2 * nch, 4 * sub, DC), F32),
            pltpu.VMEM((HALVES, 4 * sub, 2 * hid), BF),
            pltpu.VMEM((units, 4, 2 * sub, LN), BF),
            pltpu.VMEM((units, 4, 2 * sub, LN), BF),
            pltpu.VMEM((units, nk, tile, LN), BF),
            pltpu.VMEM((HALVES, 2, ih * patches, cols), BF),
            pltpu.VMEM((units, nk, tile, LN), BF),
            dma((images,)),
            dma((6,)),
            dma((3,)),
            dma((3,)),
            dma,
            dma((units,)),
            dma,
            dma((units,)),
            dma,
            dma((units,)),
            dma,
            dma((units,)),
        ],
        compiler_params=pltpu.CompilerParams(
            collective_id=0, has_side_effects=True, vmem_limit_bytes=58 * 1024 * 1024
        ),
        name="exchange",
    )(tokens, slot_keys.T, logit_scale, up_weight, up_bias, down_weight, down_bias)


def solution(mesh):
    return jax.shard_map(
        body,
        mesh=mesh,
        in_specs=(
            P(("dp", "expert"), None, None),
            P(),
            P(),
            P("expert", None, "dp"),
            P("expert", "dp"),
            P("expert", "dp", None),
            P(),
        ),
        out_specs=P(("dp", "expert"), None, None),
        check_vma=False,
    )
```

time: 63 us -> 57.3 us (0.910)
  Pallas kernels: 60.8 us -> 55 us
    pallas_call x1, Pallas kernels: 60.8 us -> 55 us  [body(): pl.pallas_call(functools.partial(exchange_kernel, nk, nch), out_shape=plt...]
where the time goes in v3:
time: 57.3 us; the launch traced here: 57.2 us
  Pallas kernels  55 us (96%)
  local copies, waits for them, and re-layouts  1.49 us (3%)
  between operations  0.66 us (1%)
    pallas_call x1, Pallas kernels, body(): pl.pallas_call(functools.partial(exchange_kernel, nk, nch), out_shape=plt...  55 us
    unnamed x1, local copies, waits for them, and re-layouts  1.49 us

profile of v3, /device:TPU:8, one launch (start us, length us, event | category | flops | bytes accessed | tf_op | source)
XLA Modules:
  0.0 57.2 jit_solution(8119903163118044758)
XLA Ops:
  0.7 55.0 %exchange.1 = bf16[4,256,1280]{2,1,0:T(8,128)(2,1)S(1)} custom-call(bf16[4,256,1280]{2,1,0:T(8,128)(2,1)} %tok_hbm.1, bf16[64,1280]{1,0:T(8,128)(2,1)} %bitcast.1, f32[1]{0:T(128)S(6)} %copy.10.scale_hbm, bf16[1,1280,1280]{2,1,0:T(8,128)(2,1)} %up_hbm.1, bf16[1,1280]{1,0:T(2,128)(2,1)} %upb_hbm.1, bf16[1,1280,1280]{2,1,0:T(8,128)(2,1)} %down_hbm.1, ...), custom_call_target="tpu_custom_call" | custom-call | tf_op jit(solution)/shard_map/exchange/pallas_call | solution.py:384
  55.7 1.5 %copy.9 = bf16[4,256,1280]{2,1,0:T(8,128)(2,1)} copy(bf16[4,256,1280]{2,1,0:T(8,128)(2,1)S(1)} %exchange.1) | data formatting | bytes 5242880

commit v4 on v3

--- a/solution.py
+++ b/solution.py
@@ -22,6 +22,14 @@
 
 def dot(a, b):
     return jnp.dot(a, b, preferred_element_type=F32)
+
+
+def offsets(nk):
+    ny, nz = (4, 8) if nk == 32 else (1, nk)
+    hops = lambda d, n: min(d, n - d)
+    near = [(1, 2), (3, 6), (2, 1), (2, 7)] if nk == 32 else []
+    key = lambda o: (hops(o[0], ny) + hops(o[1], nz), o not in near, hops(o[1], nz))
+    return ny, nz, sorted([(dy, dz) for dy in range(ny) for dz in range(nz)], key=key)
 
 
 def exchange_kernel(
@@ -54,6 +62,7 @@
     rows,
     pre,
     hidden,
+    joined,
     part_s,
     part_r,
     fin,
@@ -75,7 +84,7 @@
     images, patches, width = tok.shape
     ih = images // HALVES
     tile = 4 * ih
-    sub = nk * ih
+    sub = nk // 2 * ih
     block = 2 * sub
     n_exp = keys_ref.shape[0]
     units = HALVES * nch
@@ -88,8 +97,15 @@
     core = dp + 1 - 2 * lax.rem(dp, 2)
     members = ((dp, own), (dp, flip), (far, flip), (far, own))
 
-    def peer(step):
-        k = lax.rem(k_own + step, nk)
+    ny, nz, order = offsets(nk)
+    y_own, z_own = lax.div(k_own, nz), lax.rem(k_own, nz)
+    near = nk // 2
+
+    def peer(pos, sign=1):
+        dy, dz = order[pos]
+        y = lax.rem(y_own + (sign * dy) % ny, ny)
+        z = lax.rem(z_own + (sign * dz) % nz, nz)
+        k = y * nz + z
         return k, {"dp": dp, "expert": 2 * k + parity}
 
     tok_in = [
@@ -108,13 +124,13 @@
 
     barrier = pltpu.get_barrier_semaphore()
 
-    def greet(step, _):
-        _, where = peer(step)
+    def greet(pos, _):
+        _, where = peer(pos)
         pl.semaphore_signal(barrier, inc=1, device_id=where, device_id_type=MESH)
         return 0
 
-    for step in range(1, nk):
-        greet(step, 0)
+    for pos in reversed(range(1, nk)):
+        greet(pos, 0)
     for d, e in members[1:]:
         pl.semaphore_signal(barrier, inc=1, device_id={"dp": d, "expert": e}, device_id_type=MESH)
     pl.semaphore_signal(barrier, inc=1, device_id={"dp": core, "expert": own}, device_id_type=MESH)
@@ -179,63 +195,85 @@
         half = lax.div(u, nch)
         return half, u - half * nch
 
-    def send_tiles(buf, dst, u, s_sem, r_sem):
-        def one(step, _):
-            k, where = peer(step)
-            pltpu.make_async_remote_copy(
-                src_ref=buf.at[u, k],
-                dst_ref=dst.at[u, k_own],
-                send_sem=s_sem,
-                recv_sem=r_sem.at[u],
-                device_id=where,
-                device_id_type=MESH,
-            ).start()
-            return 0
-
-        for step in range(1, nk):
-            one(step, 0)
-
-    def dispatch(u):
+    def groups(part):
+        return range(nk - 1, near - 1, -1) if part else range(near - 1, 0, -1)
+
+    def compute_slots(u):
         half, c = of(u)
         ts = tok[pl.ds(half * ih, ih), :, lanes(c)].reshape(ih * patches, DC)
         s = dot(disp_t[half, 0], ts[:, :LN]) + dot(disp_t[half, 1], ts[:, LN:])
         slots_s[u] = s.reshape(nk, tile, LN).astype(BF)
-        slots_r[u, k_own] = slots_s[u, k_own]
-        send_tiles(slots_s, slots_r, u, s1_sem, r1_sem)
-
-    def to_member(src_ref, dst_ref, u, m, s_sem, r_sem):
+        slots_r[u, 0] = slots_s[u, k_own]
+
+    def send_slots(u, part):
+        for pos in groups(part):
+            k, where = peer(pos)
+            pltpu.make_async_remote_copy(
+                src_ref=slots_s.at[u, k],
+                dst_ref=slots_r.at[u, pos],
+                send_sem=s1_sem,
+                recv_sem=r1_sem.at[u, part],
+                device_id=where,
+                device_id_type=MESH,
+            ).start()
+
+    def dispatch_near(u):
+        compute_slots(u)
+        send_slots(u, 0)
+
+    def dispatch_far(u):
+        send_slots(u, 1)
+
+    def dispatch(u):
+        compute_slots(u)
+        send_slots(u, 1)
+        send_slots(u, 0)
+
+    def send_back(u, part):
+        for pos in groups(part):
+            k, where = peer(pos, -1)
+            pltpu.make_async_remote_copy(
+                src_ref=fin.at[u, pos],
+                dst_ref=got.at[u, k_own],
+                send_sem=s4_sem,
+                recv_sem=r4_sem.at[u],
+                device_id=where,
+                device_id_type=MESH,
+            ).start()
+
+    def to_member(src_ref, dst_ref, m, s_sem, r_sem):
         d, e = members[m]
         return pltpu.make_async_remote_copy(
             src_ref=src_ref,
-            dst_ref=dst_ref.at[u, m],
+            dst_ref=dst_ref,
             send_sem=s_sem,
-            recv_sem=r_sem.at[u],
+            recv_sem=r_sem,
             device_id={"dp": d, "expert": e},
             device_id_type=MESH,
         )
 
-    def wait_tiles(buf, u, r_sem):
-        view = buf.at[u, pl.ds(0, nk - 1)]
-        pltpu.make_async_copy(view, view, r_sem.at[u]).wait()
-
-    def wait_members(buf, u, r_sem):
-        view = buf.at[u, pl.ds(1, 3)]
-        pltpu.make_async_copy(view, view, r_sem.at[u]).wait()
-
-    def spread_x(u):
-        wait_tiles(slots_r, u, r1_sem)
-        moved = dot(perm[...], slots_r[u].reshape(2 * block, LN)).astype(BF)
-        rows[u, 0] = moved[:block]
-        rows[u, 4] = moved[block:]
+    def spread_x(u, part):
+        count = near if part else near - 1
+        view = slots_r.at[u, pl.ds(nk - count if part else 1, count)]
+        if count:
+            pltpu.make_async_copy(view, view, r1_sem.at[u, part]).wait()
+        tiles = slots_r[u, pl.ds(part * near, near)].reshape(2 * block, LN)
+        moved = dot(perm[...], tiles).astype(BF)
+        rows[u, part, 0] = moved[:block]
+        rows[u, part, 4] = moved[block:]
         for m, piece in ((3, 0), (1, 4), (2, 4)):
-            to_member(rows.at[u, piece], rows, u, m, s2_sem, r2_sem).start()
+            to_member(
+                rows.at[u, part, piece], rows.at[u, part, m], m, s2_sem, r2_sem.at[u]
+            ).start()
 
     def up(u):
         half, c = of(u)
-        wait_members(rows, u, r2_sem)
+        view = rows.at[u, pl.ds(0, 2), pl.ds(1, 3)]
+        pltpu.make_async_copy(view, view, r2_sem.at[u]).wait()
         x = jnp.concatenate(
-            [rows[u, pl.ds(0, 4), pl.ds(0, sub)], rows[u, pl.ds(0, 4), pl.ds(sub, sub)]], axis=2
-        ).reshape(4 * sub, DC)
+            [rows[u, :, pl.ds(0, 4), pl.ds(0, sub)], rows[u, :, pl.ds(0, 4), pl.ds(sub, sub)]],
+            axis=3,
+        ).reshape(8 * sub, DC)
         for j in range(2 * nch):
             which, at = divmod(j, nch)
             pre[half, j] += dot(x, wup[which, lanes(c), at * DC : (at + 1) * DC])
@@ -251,31 +289,63 @@
 
             lax.fori_loop(0, nch, one, 0)
 
+    def join(half):
+        for c in range(nch):
+            view = rows.at[half * nch + c, pl.ds(0, 2), pl.ds(1, 3)]
+            pltpu.make_async_copy(view, view, r2_sem.at[half * nch + c]).wait()
+        pieces = [
+            rows[half * nch + c, :, pl.ds(0, 4), pl.ds(cc * sub, sub)]
+            for c in range(nch)
+            for cc in range(2)
+        ]
+        joined[...] = jnp.concatenate(pieces, axis=3).reshape(8 * sub, width)
+
+    def up_and_activate(half, which, bias_ref):
+        for j in range(nch):
+            cols = slice(j * DC, (j + 1) * DC)
+            v = dot(joined[...], wup[which, :, cols]) + bias_ref[:, cols].astype(F32)
+            h = 0.5 * v * (1.0 + lax.erf(v * (2.0**-0.5)))
+            hidden[half, :, which * width + j * DC : which * width + (j + 1) * DC] = h.astype(BF)
+
     def down(u):
         half, c = of(u)
-        p = dot(hidden[half, :, pl.ds(0, width)], wdown[0, :, lanes(c)])
-        p = p + dot(hidden[half, :, pl.ds(width, width)], wdown[1, :, lanes(c)])
-        p = p.astype(BF)
-        part_s[u, :, pl.ds(0, sub)] = p[:, :LN].reshape(4, sub, LN)
-        part_s[u, :, pl.ds(sub, sub)] = p[:, LN:].reshape(4, sub, LN)
+        p = dot(hidden[half], wdown[:, :, lanes(c)].reshape(2 * width, DC)).astype(BF)
+        part_s[u, :, :, pl.ds(0, sub)] = p[:, :LN].reshape(2, 4, sub, LN)
+        part_s[u, :, :, pl.ds(sub, sub)] = p[:, LN:].reshape(2, 4, sub, LN)
+
+    def send_part(u, part):
         for m in (3, 1, 2):
-            to_member(part_s.at[u, m], part_r, u, m, s3_sem, r3_sem).start()
-
-    def finish(u):
+            to_member(
+                part_s.at[u, part, m], part_r.at[u, part, m], m, s3_sem, r3_sem.at[u, part]
+            ).start()
+
+    def down_both(u):
+        down(u)
+        send_part(u, 1)
+        send_part(u, 0)
+
+    def down_far(u):
+        down(u)
+        send_part(u, 1)
+
+    def finish(u, part):
         half, c = of(u)
-        wait_members(part_r, u, r3_sem)
-        mine = part_s[u, 0].astype(F32) + part_r[u, 3].astype(F32)
-        other = part_r[u, 1].astype(F32) + part_r[u, 2].astype(F32)
+        view = part_r.at[u, part, pl.ds(1, 3)]
+        pltpu.make_async_copy(view, view, r3_sem.at[u, part]).wait()
+        mine = part_s[u, part, 0].astype(F32) + part_r[u, part, 3].astype(F32)
+        other = part_r[u, part, 1].astype(F32) + part_r[u, part, 2].astype(F32)
         total = jnp.concatenate([mine, other], axis=0) + bias_rows[c].astype(F32)
-        moved = dot(permt[...], total.astype(BF))
-        fin[u] = moved.reshape(nk, tile, LN).astype(BF)
-        got[u, k_own] = fin[u, k_own]
-        send_tiles(fin, got, u, s4_sem, r4_sem)
+        moved = dot(permt[...], total.astype(BF)).reshape(near, tile, LN).astype(BF)
+        fin[u, pl.ds(part * near, near)] = moved
+        if part == 0:
+            got[u, k_own] = fin[u, 0]
+        send_back(u, part)
 
     def mix(u):
         half, c = of(u)
-        wait_tiles(got, u, r4_sem)
-        back = got[u].reshape(2 * block, LN)
+        view = got.at[u, pl.ds(0, nk - 1)]
+        pltpu.make_async_copy(view, view, r4_sem.at[u]).wait()
+        back = got[u].reshape(nk * tile, LN)
         for at in range(ih):
             for cc in range(2):
                 mixed = dot(comb[half, cc, pl.ds(at * patches, patches), :], back)
@@ -306,7 +376,7 @@
         permt[...] = (source(perm.shape, 1) == iota(perm.shape, 0)).astype(BF)
         for half in range(HALVES):
             for j in range(2 * nch):
-                pre[half, j] = jnp.zeros((4 * sub, DC), F32)
+                pre[half, j] = jnp.zeros((8 * sub, DC), F32)
 
     def prepare_later():
         lax.fori_loop(0, images, mix_weights, 0)
@@ -327,33 +397,64 @@
 
         lax.fori_loop(first, last, one, 0)
 
-    ahead = units - 3
     sends_w[2].start()
-    run(0, nch, (dispatch, 0))
-    soften(range(ih, images))
-    run(nch, ahead, (dispatch, 0))
+    run(0, nch, (dispatch_near, 0))
+    run(0, nch, (dispatch_far, 0))
     sends_w[0].start()
     sends_w[1].start()
     prepare()
+    soften(range(ih, images))
+
+    def spread_near(u):
+        spread_x(u, 0)
+
+    def spread_far(u):
+        spread_x(u, 1)
+
+    def spread_both(u):
+        spread_x(u, 1)
+        spread_x(u, 0)
+
+    run(0, nch, (dispatch, nch), (spread_near, 0))
     prepare_later()
-    run(0, 3, (spread_x, 0), (dispatch, ahead))
     up_in.wait()
     sends_w[0].wait_recv()
-    run(0, nch, (spread_x, 3), (up, 0))
+    run(0, 3, (spread_far, 0))
+    run(0, 2, (spread_far, 3), (up, 0))
+    run(0, 3, (spread_both, nch), (up, 2))
     upb_in.wait()
     sends_w[2].wait_recv()
-    spread_x(nch + 3)
+    spread_both(nch + 3)
     activate(0)
-    spread_x(nch + 4)
+    spread_both(nch + 4)
     down_in.wait()
     sends_w[1].wait_recv()
-    run(0, nch, (down, 0))
-
-    run(0, nch, (up, nch))
-    activate(1)
-    run(0, nch, (down, nch), (finish, 0))
-    run(0, nch, (finish, nch), (mix, 0))
-    run(nch, units, (mix, 0))
+    run(0, nch, (down_both, 0))
+    def finish_near(u):
+        finish(u, 0)
+
+    def finish_far(u):
+        finish(u, 1)
+
+    def finish_both(u):
+        finish(u, 1)
+        finish(u, 0)
+
+    def finish_next(t):
+        @pl.when(t + 1 < nch)
+        def _():
+            finish_both(t + 1)
+
+    join(1)
+    up_and_activate(1, 0, upb_ref)
+    run(0, 1, (finish_both, 0))
+    up_and_activate(1, 1, bup)
+    run(0, nch, (finish_next, 0), (down_far, nch))
+    for c in range(nch):
+        send_part(nch + c, 0)
+    run(0, nch, (finish_far, nch))
+    run(0, nch, (finish_near, nch))
+    run(0, units, (mix, 0))
 
     def drain(buf, first, count, sem):
         view = buf.at[:, pl.ds(first, count)]
@@ -362,8 +463,9 @@
     for copy in sends_w:
         copy.wait_send()
     drain(slots_s, 0, nk - 1, s1_sem)
-    drain(rows, 1, 3, s2_sem)
-    drain(part_s, 1, 3, s3_sem)
+    for buf, sem in ((rows, s2_sem), (part_s, s3_sem)):
+        view = buf.at[:, :, pl.ds(1, 3)]
+        pltpu.make_async_copy(view, view, sem).wait()
     drain(fin, 0, nk - 1, s4_sem)
 
 
@@ -375,7 +477,7 @@
     ih = images // HALVES
     tile = 4 * ih
     cols = nk * tile
-    sub = nk * ih
+    sub = nk // 2 * ih
     units = HALVES * nch
     hid = up_weight.shape[2]
     dma = pltpu.SemaphoreType.DMA
@@ -403,11 +505,12 @@
             pltpu.VMEM((nch, 4 * sub, LN), BF),
             pltpu.VMEM((units, nk, tile, LN), BF),
             pltpu.VMEM((units, nk, tile, LN), BF),
-            pltpu.VMEM((units, 5, 2 * sub, LN), BF),
-            pltpu.VMEM((HALVES, 2 * nch, 4 * sub, DC), F32),
-            pltpu.VMEM((HALVES, 4 * sub, 2 * hid), BF),
-            pltpu.VMEM((units, 4, 2 * sub, LN), BF),
-            pltpu.VMEM((units, 4, 2 * sub, LN), BF),
+            pltpu.VMEM((units, 2, 5, 2 * sub, LN), BF),
+            pltpu.VMEM((HALVES, 2 * nch, 8 * sub, DC), F32),
+            pltpu.VMEM((HALVES, 8 * sub, 2 * hid), BF),
+            pltpu.VMEM((8 * sub, width), BF),
+            pltpu.VMEM((units, 2, 4, 2 * sub, LN), BF),
+            pltpu.VMEM((units, 2, 4, 2 * sub, LN), BF),
             pltpu.VMEM((units, nk, tile, LN), BF),
             pltpu.VMEM((HALVES, 2, ih * patches, cols), BF),
             pltpu.VMEM((units, nk, tile, LN), BF),
@@ -416,11 +519,11 @@
             dma((3,)),
             dma((3,)),
             dma,
-            dma((units,)),
+            dma((units, 2)),
             dma,
             dma((units,)),
             dma,
-            dma((units,)),
+            dma((units, 2)),
             dma,
             dma((units,)),
         ],

time: 57.3 us -> 56.1 us (0.979)
  Pallas kernels: 55 us -> 53.4 us
    pallas_call x1, Pallas kernels: 55 us -> 53.4 us  [body(): pl.pallas_call(functools.partial(exchange_kernel, nk, nch), out_shape=plt...]
where the time goes in v4:
time: 56.1 us; the launch traced here: 55.5 us
  Pallas kernels  53.4 us (95%)
  local copies, waits for them, and re-layouts  1.49 us (3%)
  between operations  0.66 us (1%)
    pallas_call x1, Pallas kernels, body(): pl.pallas_call(functools.partial(exchange_kernel, nk, nch), out_shape=plt...  53.4 us
    unnamed x1, local copies, waits for them, and re-layouts  1.49 us

profile of v4, /device:TPU:8, one launch (start us, length us, event | category | flops | bytes accessed | tf_op | source)
XLA Modules:
  0.0 55.5 jit_solution(4779120797242993349)
XLA Ops:
  0.7 53.4 %exchange.1 = bf16[4,256,1280]{2,1,0:T(8,128)(2,1)S(1)} custom-call(bf16[4,256,1280]{2,1,0:T(8,128)(2,1)} %tok_hbm.1, bf16[64,1280]{1,0:T(8,128)(2,1)} %bitcast.1, f32[1]{0:T(128)S(6)} %copy.10.scale_hbm, bf16[1,1280,1280]{2,1,0:T(8,128)(2,1)} %up_hbm.1, bf16[1,1280]{1,0:T(2,128)(2,1)} %upb_hbm.1, bf16[1,1280,1280]{2,1,0:T(8,128)(2,1)} %down_hbm.1, ...), custom_call_target="tpu_custom_call" | custom-call | tf_op jit(solution)/shard_map/exchange/pallas_call | solution.py:486
  54.0 1.5 %copy.9 = bf16[4,256,1280]{2,1,0:T(8,128)(2,1)} copy(bf16[4,256,1280]{2,1,0:T(8,128)(2,1)S(1)} %exchange.1) | data formatting | bytes 5242880

commit v5 on v4

--- a/solution.py
+++ b/solution.py
@@ -351,6 +351,20 @@
                 mixed = dot(comb[half, cc, pl.ds(at * patches, patches), :], back)
                 out_ref[half * ih + at, :, lane_tile(c, cc)] = mixed.astype(BF)
 
+    def mix_pair(t):
+        half = HALVES - 1
+        c = 2 * t
+        u = half * nch + c
+        for v in range(2):
+            view = got.at[u + v, pl.ds(0, nk - 1)]
+            pltpu.make_async_copy(view, view, r4_sem.at[u + v]).wait()
+        back = jnp.concatenate([got[u + v].reshape(nk * tile, LN) for v in range(2)], axis=1)
+        for at in range(ih):
+            for cc in range(2):
+                mixed = dot(comb[half, cc, pl.ds(at * patches, patches), :], back).astype(BF)
+                out_ref[half * ih + at, :, lane_tile(c, cc)] = mixed[:, :LN]
+                out_ref[half * ih + at, :, lane_tile(c + 1, cc)] = mixed[:, LN:]
+
     def mix_weights(i, _):
         logits = scores[pl.ds(pl.multiple_of(i * patches, patches), patches), :]
         half = lax.div(i, ih)
@@ -454,7 +468,9 @@
         send_part(nch + c, 0)
     run(0, nch, (finish_far, nch))
     run(0, nch, (finish_near, nch))
-    run(0, units, (mix, 0))
+    run(0, nch, (mix, 0))
+    run(0, nch // 2, (mix_pair, 0))
+    run(units - nch % 2, units, (mix, 0))
 
     def drain(buf, first, count, sem):
         view = buf.at[:, pl.ds(first, count)]

time: 56.1 us -> 56.1 us (level)
  no operation moved by 1% of the time
where the time goes in v5:
time: 56.1 us; the launch traced here: 55.4 us
  Pallas kernels  53.3 us (95%)
  local copies, waits for them, and re-layouts  1.49 us (3%)
  between operations  0.66 us (1%)
    pallas_call x1, Pallas kernels, body(): pl.pallas_call(functools.partial(exchange_kernel, nk, nch), out_shape=plt...  53.3 us
    unnamed x1, local copies, waits for them, and re-layouts  1.49 us

profile of v5, /device:TPU:8, one launch (start us, length us, event | category | flops | bytes accessed | tf_op | source)
XLA Modules:
  0.0 55.4 jit_solution(12495503317032117633)
XLA Ops:
  0.7 53.3 %exchange.1 = bf16[4,256,1280]{2,1,0:T(8,128)(2,1)S(1)} custom-call(bf16[4,256,1280]{2,1,0:T(8,128)(2,1)} %tok_hbm.1, bf16[64,1280]{1,0:T(8,128)(2,1)} %bitcast.1, f32[1]{0:T(128)S(6)} %copy.10.scale_hbm, bf16[1,1280,1280]{2,1,0:T(8,128)(2,1)} %up_hbm.1, bf16[1,1280]{1,0:T(2,128)(2,1)} %upb_hbm.1, bf16[1,1280,1280]{2,1,0:T(8,128)(2,1)} %down_hbm.1, ...), custom_call_target="tpu_custom_call" | custom-call | tf_op jit(solution)/shard_map/exchange/pallas_call | solution.py:502
  53.9 1.5 %copy.9 = bf16[4,256,1280]{2,1,0:T(8,128)(2,1)} copy(bf16[4,256,1280]{2,1,0:T(8,128)(2,1)S(1)} %exchange.1) | data formatting | bytes 5242880
